TPU v7x, 128 devices: a whole 4x4x4 slice. The times are simulated.
128 devices in a mesh: dp: 64 (over z, y, x), mp: 2 (over core).
Axes of the slice: x: 4, y: 4, z: 4, core: 2. Of those that a mesh axis runs over, the one named last changes fastest.
Arguments:
- pixels: bfloat16 [128, 512, 768], P(('dp', 'mp')), may hold values from -6 to 6
- counts: int32 [64, 2], P('dp'), may hold values from 128 to 512
- owner: int32 [64, 2], P('dp'), may hold values from 0 to 1, each once within a row
- embed_weight: bfloat16 [768, 1024], P('dp', 'mp'), may hold values from -0.21875 to 0.21875
- w_qkv: bfloat16 [3, 1024, 1024], P(None, 'dp', 'mp'), may hold values from -0.8 to 0.8
- w_out: bfloat16 [1024, 1024], P('mp', 'dp'), may hold values from -0.1875 to 0.1875
- w_up: bfloat16 [1024, 4096], P('dp', 'mp'), may hold values from -0.1875 to 0.1875
- w_down: bfloat16 [4096, 1024], P('mp', 'dp'), may hold values from -0.09375 to 0.09375
- ln1_gain: float32 [1024], replicated, may hold values from 0.25 to 1.75
- ln2_gain: float32 [1024], replicated, may hold values from 0.25 to 1.75
- targets: bfloat16 [64, 2, 512, 1024], P('dp', None, 'mp'), may hold values from -20 to 20
Outputs:
- encoded: bfloat16 [64, 2, 512, 1024], P('dp', None, 'mp')
- mean_loss: float32 [], replicated
Inputs may be any that keep to these rules, and one draw needn't show every extreme that they name: counts[g, r] is the number of valid patches at the start of image g * 2 + r; the remaining patch slots are padding. Each row owner[g, :] is a permutation of 0 to 2 - 1, so every held image is encoded once.
All inputs are finite; a program needn't handle non-finite values.
Results may differ from a plain program's by a relative error of at most 0.014.
Values may be sent and summed in bfloat16 or wider, within the bound.
A program may use at most 128 MiB of HBM per device.

v0:
```python
import jax
import jax.numpy as jnp
from jax import lax
from jax.experimental import pallas as pl
from jax.experimental.pallas import tpu as pltpu
from jax.sharding import Mesh
from jax.sharding import PartitionSpec as P

D = 1024
HEAD = 64
DP = ("dp_0", "dp_1", "dp_2")
DP_MP = ("dp_0", "dp_1", "dp_2", "mp")
MESH = pl.DeviceIdType.MESH
TILE = 128
ORDERS = ((2, 1, 0), (1, 0, 2), (0, 2, 1))
BATCHES = ((6, 5, 5), (4, 4, 4), (4, 4, 4), (4, 4, 4))
UP_TILES = (4, 6, 6)
COLUMNS = TILE * sum(sum(b) for b in BATCHES)


def spans():
    out, at = [], 0
    for batch in BATCHES:
        row = []
        for tiles in batch:
            row.append((at * TILE, tiles * TILE))
            at += tiles
        out.append(row)
    return out


SPANS = spans()


class Gather:

    def __init__(self, whole_ref, send_sems, recv_sems):
        self.whole = whole_ref
        self.send, self.recv = send_sems, recv_sems
        self.me = [lax.axis_index(a) for a in DP]
        self.half = lax.axis_index("mp")
        self.copies = {}
        self.count = 0
        self.started = []

    def region(self, order, phase, coord, start, size):
        at = [None, None, None]
        for i in range(3):
            axis = order[i]
            at[axis] = pl.ds(0, 4) if i < phase else (coord if i == phase else self.me[axis])
        return self.whole.at[self.half, at[0], at[1], at[2], :, pl.ds(start, size)]

    def copy(self, key, src, dst, device):
        made = pltpu.make_async_remote_copy(
            src_ref=src,
            dst_ref=dst,
            send_sem=self.send.at[self.count],
            recv_sem=self.recv.at[self.count],
            device_id=device,
            device_id_type=MESH,
        )
        self.count += 1
        made.start()
        self.started.append(made)
        self.copies[key] = made

    def ring(self, batch, colour, phase):
        order = ORDERS[colour]
        axis = order[phase]
        mine = self.me[axis]
        right, left = lax.rem(mine + 1, 4), lax.rem(mine + 3, 4)
        return order, DP[axis], mine, right, left

    def step_a(self, batch, phase):
        for colour in range(3):
            if phase > 0:
                for side in "rl":
                    self.copies[batch, colour, phase - 1, "b", side].wait_recv()
            order, name, mine, right, left = self.ring(batch, colour, phase)
            start, size = SPANS[batch][colour]
            block = self.region(order, phase, mine, start, size)
            self.copy((batch, colour, phase, "a", "r"), block, block, {name: right})
            self.copy((batch, colour, phase, "a", "l"), block, block, {name: left})
            if phase == 2:
                self.across(batch, colour, mine)

    def step_b(self, batch, phase):
        for colour in range(3):
            for side in "rl":
                self.copies[batch, colour, phase, "a", side].wait_recv()
            order, name, mine, right, left = self.ring(batch, colour, phase)
            start, size = SPANS[batch][colour]
            first = size // TILE // 2 * TILE
            from_left = self.region(order, phase, left, start, first)
            from_right = self.region(order, phase, right, start + first, size - first)
            self.copy((batch, colour, phase, "b", "r"), from_left, from_left, {name: right})
            self.copy((batch, colour, phase, "b", "l"), from_right, from_right, {name: left})
            if phase == 2:
                self.across(batch, colour, left)
                self.across(batch, colour, right)

    def across(self, batch, colour, coord):
        start, size = SPANS[batch][colour]
        block = self.region(ORDERS[colour], 2, coord, start, size)
        kind = sum(1 for k in self.copies if k[:2] == (batch, colour) and k[2] == "x")
        self.copy((batch, colour, "x", kind), block, block, {"mp": 1 - self.half})

    def finish(self, batch):
        for colour in range(3):
            for side in "rl":
                self.copies[batch, colour, 2, "b", side].wait_recv()
            mine = self.me[ORDERS[colour][2]]
            self.across(batch, colour, lax.rem(mine + 2, 4))

    def arrived(self, batch):
        for colour in range(3):
            for kind in range(4):
                self.copies[batch, colour, "x", kind].wait_recv()

    def drain(self):
        for made in self.started:
            made.wait_send()


def greet():
    barrier = pltpu.get_barrier_semaphore()
    count = 0
    for name in DP:
        mine = lax.axis_index(name)
        for step in (1, 2, 3):
            pl.semaphore_signal(
                barrier, inc=1, device_id={name: lax.rem(mine + step, 4)}, device_id_type=MESH
            )
            count += 1
    pl.semaphore_signal(
        barrier, inc=1, device_id={"mp": 1 - lax.axis_index("mp")}, device_id_type=MESH
    )
    pl.semaphore_wait(barrier, count + 1)


def layer_norm(inputs, gains):
    average = jnp.mean(inputs, axis=-1, keepdims=True)
    centred = inputs - average
    spread = jnp.mean(centred * centred, axis=-1, keepdims=True)
    return centred * lax.rsqrt(spread + 1e-06) * gains


def dot(a, b):
    return jnp.dot(a, b, preferred_element_type=jnp.float32)


def dot_t(a, b):
    return lax.dot_general(a, b, (((1,), (1,)), ((), ())), preferred_element_type=jnp.float32)


BF = jnp.bfloat16
N_COPIES = len(BATCHES) * 3 * 16
ROWS = 512
OWN = 256


def encode_kernel(
    counts,
    owner,
    picture,
    embed,
    w_qkv,
    w_out,
    w_up,
    w_down,
    gain1,
    gain2,
    targets,
    encoded,
    loss,
    whole,
    spread,
    tokens,
    normed,
    queries,
    key_rows,
    value_rows,
    attended,
    total,
    sending,
    by_image,
    sums,
    send_sems,
    recv_sems,
    end_send,
    end_recv,
):
    half = lax.axis_index("mp")
    me = [lax.axis_index(a) for a in DP]
    eye = (
        lax.broadcasted_iota(jnp.int32, (16, 16), 0) == lax.broadcasted_iota(jnp.int32, (16, 16), 1)
    ).astype(BF)

    def place(start, value):
        whole[half, me[0], me[1], me[2], :, pl.ds(start, value.shape[1])] = value

    place(0, jnp.concatenate([embed[...].astype(jnp.float32), jnp.zeros((4, 512), jnp.float32)], 0).astype(BF))
    for i in range(3):
        place(512 * (i + 1), w_qkv[i])
    place(2048, dot_t(eye, w_out[...]).astype(BF))
    at, hidden_at = 2560, 0
    for tiles in UP_TILES:
        size = tiles * TILE
        place(at, w_up[:, pl.ds(hidden_at, size)])
        place(at + size, dot_t(eye, w_down[pl.ds(hidden_at, size), :]).astype(BF))
        at += 2 * size
        hidden_at += size
    greet()
    g = Gather(whole, send_sems, recv_sems)

    def weights(h, start, size):
        return whole[h, :, :, :, :, pl.ds(start, size)].reshape(D, size)

    for b in range(4):
        g.step_a(b, 0)
    from_px = lax.broadcasted_iota(jnp.int32, (768, D), 0)
    column = lax.broadcasted_iota(jnp.int32, (768, D), 1)
    within = lax.bitwise_and(column, 15)
    to_px = lax.shift_right_logical(column, 4) * 12 + within
    pick = jnp.where((from_px == to_px) & (within < 12), 1.0, 0.0).astype(BF)
    spread[...] = dot(picture[...], pick).astype(BF)
    for b in range(4):
        g.step_b(b, 0)
    g.step_a(0, 1)
    g.step_a(1, 1)
    g.step_b(0, 1)
    g.step_a(0, 2)
    g.step_b(1, 1)
    g.step_a(2, 1)
    g.step_b(0, 2)
    g.step_b(2, 1)
    g.step_a(1, 2)
    g.step_a(3, 1)
    g.finish(0)
    g.arrived(0)
    for h in range(2):
        tokens[:, pl.ds(512 * h, 512)] = dot(spread[...], weights(h, 0, 512)).astype(BF)
    normed[...] = layer_norm(tokens[...].astype(jnp.float32), gain1[...]).astype(BF)
    g.step_b(1, 2)
    g.step_b(3, 1)
    g.step_a(2, 2)
    for i, (ref, factor) in enumerate(((queries, HEAD ** (-0.5)), (key_rows, 1.0), (value_rows, 1.0))):
        for h in range(2):
            part = dot(normed[...], weights(h, 512 * (i + 1), 512))
            if factor != 1.0:
                part = part * factor
            part = part.astype(BF)
            for j in range(4):
                ref[4 * h + j] = part[:, 128 * j : 128 * (j + 1)]
    g.finish(1)
    length = counts[0, half]
    key_id = lax.broadcasted_iota(jnp.int32, (1, ROWS), 1)
    bias = jnp.where(key_id < length, 0.0, -1e30)
    low = lax.broadcasted_iota(jnp.int32, (ROWS, 128), 1) < HEAD

    def pair(i, carry):
        q, k, v = queries[i], key_rows[i], value_rows[i]
        none, one = jnp.zeros_like(q), jnp.ones_like(v)

        def head(q_part, v_part):
            scores = dot_t(q_part, k) + bias
            expo = jnp.exp(scores - jnp.max(scores, axis=-1, keepdims=True))
            return dot(expo.astype(BF), v_part)

        first = head(jnp.where(low, q, none), jnp.where(low, v, one))
        second = head(jnp.where(low, none, q), jnp.where(low, one, v))
        values = jnp.where(low, first, second)
        row_sums = pltpu.roll(jnp.where(low, second, first), HEAD, 1)
        attended[i] = (values / row_sums).astype(BF)
        return carry

    lax.fori_loop(0, 3, pair, 0)
    g.step_b(2, 2)
    g.step_a(3, 2)
    lax.fori_loop(3, 8, pair, 0)
    g.finish(2)
    residual = tokens[...].astype(jnp.float32)
    g.arrived(1)
    for h in range(2):
        mixed = jnp.concatenate([attended[4 * h + j] for j in range(4)], axis=1)
        residual = residual + dot_t(mixed, weights(h, 2048, 512))
    total[...] = residual
    normed[...] = layer_norm(residual, gain2[...]).astype(BF)
    g.step_b(3, 2)

    def mlp(rows, h, at, size):
        hidden = dot(normed[rows, :], weights(h, at, size))
        hidden = hidden * 0.5 * (1.0 + lax.erf(hidden * (0.5**0.5)))
        return dot_t(hidden.astype(BF), weights(h, at + size, size))

    everything = pl.ds(0, ROWS)
    total[...] += mlp(everything, 0, 2560, 512)
    total[...] += mlp(everything, 1, 2560, 512)
    g.finish(3)
    g.arrived(2)
    total[...] += mlp(everything, 0, 3584, 768)
    total[...] += mlp(everything, 1, 3584, 768)
    g.arrived(3)
    other = 1 - half
    for piece, mine in ((other, False), (half, True)):
        rows = pl.ds(pl.multiple_of(piece * OWN, OWN), OWN)
        result = (total[rows, :] + mlp(rows, 0, 5120, 768) + mlp(rows, 1, 5120, 768)).astype(BF)
        if mine:
            by_image[half] = result
        else:
            sending[...] = result
            exchange = pltpu.make_async_remote_copy(
                src_ref=sending,
                dst_ref=by_image.at[half],
                send_sem=end_send.at[0],
                recv_sem=end_recv.at[0],
                device_id={"mp": other},
                device_id_type=MESH,
            )
            exchange.start()
    exchange.wait_recv()
    row_id = half * OWN + lax.broadcasted_iota(jnp.int32, (OWN, 1), 0)
    squares = jnp.zeros((8, 128), jnp.float32)
    number = jnp.zeros((8, 128), jnp.float32)
    for step in range(2):
        source = owner[0, step]
        valid = jnp.where(source == 0, counts[0, 0], counts[0, 1])
        rows = jnp.where(source == 0, by_image[0].astype(jnp.float32), by_image[1].astype(jnp.float32))
        encoded[step] = rows.astype(BF)
        misfit = rows - targets[step].astype(jnp.float32)
        misfit = jnp.where(row_id < valid, misfit * misfit, 0.0)
        squares = squares + misfit.reshape(OWN // 8, 8, 8, 128).sum(axis=(0, 2))
        number = number + jnp.clip(valid - half * OWN, 0, OWN).astype(jnp.float32)
    both = jnp.concatenate([squares, number], 0)
    at = 1
    lines = [("mp", 2, half)] + [(name, 4, mine) for name, mine in zip(DP, me)]
    for stage, (name, members, mine) in enumerate(lines):
        sums[stage, mine] = both
        sent = []
        for step in range(1, members):
            made = pltpu.make_async_remote_copy(
                src_ref=sums.at[stage, mine],
                dst_ref=sums.at[stage, mine],
                send_sem=end_send.at[at],
                recv_sem=end_recv.at[at],
                device_id={name: lax.rem(mine + step, members)},
                device_id_type=MESH,
            )
            made.start()
            sent.append(made)
            at += 1
        for made in sent:
            made.wait_recv()
        both = sums[stage, 0]
        for other_member in range(1, members):
            both = both + sums[stage, other_member]
        for made in sent:
            made.wait_send()
    mean = jnp.sum(both[:8]) / (D * jnp.max(both[8:]))
    loss[...] = jnp.full((8, 128), mean, jnp.float32)
    exchange.wait_send()
    g.drain()


def on_device(
    pixels, counts, owner, embed_weight, w_qkv, w_out, w_up, w_down, ln1_gain, ln2_gain, targets
):
    vmem = pl.BlockSpec(memory_space=pltpu.VMEM)
    smem = pl.BlockSpec(memory_space=pltpu.SMEM)
    encoded, loss = pl.pallas_call(
        encode_kernel,
        out_shape=(
            jax.ShapeDtypeStruct((2, OWN, D), BF),
            jax.ShapeDtypeStruct((8, 128), jnp.float32),
        ),
        in_specs=[smem, smem] + [vmem] * 9,
        out_specs=(vmem, vmem),
        scratch_shapes=[
            pltpu.VMEM((2, 4, 4, 4, 16, COLUMNS), BF),
            pltpu.VMEM((ROWS, D), BF),
            pltpu.VMEM((ROWS, D), BF),
            pltpu.VMEM((ROWS, D), BF),
            pltpu.VMEM((8, ROWS, 128), BF),
            pltpu.VMEM((8, ROWS, 128), BF),
            pltpu.VMEM((8, ROWS, 128), BF),
            pltpu.VMEM((8, ROWS, 128), BF),
            pltpu.VMEM((ROWS, D), jnp.float32),
            pltpu.VMEM((OWN, D), BF),
            pltpu.VMEM((2, OWN, D), BF),
            pltpu.VMEM((4, 4, 16, 128), jnp.float32),
            pltpu.SemaphoreType.DMA((N_COPIES,)),
            pltpu.SemaphoreType.DMA((N_COPIES,)),
            pltpu.SemaphoreType.DMA((11,)),
            pltpu.SemaphoreType.DMA((11,)),
        ],
        compiler_params=pltpu.CompilerParams(
            collective_id=0, has_side_effects=True, vmem_limit_bytes=64 * 1024 * 1024 - 65536
        ),
        name="encode",
    )(
        counts,
        owner,
        pixels[0],
        embed_weight,
        w_qkv,
        w_out,
        w_up,
        w_down,
        ln1_gain[None],
        ln2_gain[None],
        targets[0],
    )
    return (encoded[None], loss[0, 0])


def solution(mesh):
    split = Mesh(mesh.devices.reshape(4, 4, 4, mesh.shape["mp"]), ("dp_0", "dp_1", "dp_2", "mp"))
    return jax.shard_map(
        on_device,
        mesh=split,
        in_specs=(
            P(DP_MP, None, None),
            P(DP, None),
            P(DP, None),
            P(DP, "mp"),
            P(None, DP, "mp"),
            P("mp", DP),
            P(DP, "mp"),
            P("mp", DP),
            P(),
            P(),
            P(DP, None, "mp", None),
        ),
        out_specs=(P(DP, None, "mp", None), P()),
        check_vma=False,
    )
```

profile of v0, /device:TPU:1, one launch (start us, length us, event | category | flops | bytes accessed | tf_op | source)
XLA Modules:
  0.0 103.7 jit_solution(12068280921113875661)
XLA Ops:
  0.6 0.0 copy-start
  0.6 1.5 %copy.13.w_out = bf16[512,16]{1,0:T(8,128)(2,1)} copy(bf16[512,16]{0,1:T(8,128)(2,1)} %param.16) | data formatting | bytes 32768 | tf_op args[5]
  2.1 0.0 copy-done
  2.1 1.0 copy.14.w_down
  3.1 97.1 %encode.1 = (bf16[2,256,1024]{2,1,0:T(8,128)(2,1)}, f32[8,128]{1,0:T(8,128)}) custom-call(s32[1,2]{1,0:T(1,128)} %counts.1, s32[1,2]{1,0:T(1,128)} %owner.1, bf16[512,768]{1,0:T(8,128)(2,1)} %bitcast.8, bf16[12,512]{1,0:T(8,128)(2,1)} %embed.1, bf16[3,16,512]{2,1,0:T(8,128)(2,1)} %w_qkv.1, bf16[512,16]{1,0:T(8,128)(2,1)} %copy.13.w_out, ...), custom_call_target="tpu_custom_call" | custom-call | tf_op jit(solution)/shard_map/encode/pallas_call | solution.py:370
  100.2 1.2 %slice.3 = f32[1,1]{1,0:T(1,128)} slice(f32[8,128]{1,0:T(8,128)} %get-tuple-element.5), slice={[0:1], [0:1]} | slice | bytes 8 | tf_op jit(solution)/shard_map/slice | solution.py:413
  101.4 2.3 %copy.16 = bf16[1,2,256,1024]{3,2,1,0:T(8,128)(2,1)} copy(bf16[1,2,256,1024]{3,2,1,0:T(8,128)(2,1)} %bitcast.7) | data formatting | bytes 2097152
Async XLA Ops:
  0.6 1.5 %copy-start = (bf16[2048,16]{0,1:T(8,128)(2,1)S(1)}, bf16[2048,16]{0,1:T(8,128)(2,1)}, u32[]{:S(2)}) copy-start(bf16[2048,16]{0,1:T(8,128)(2,1)} %param.18) | copy-start | bytes 196612
where the time goes:
time: 105 us; the launch traced here: 104 us
  Pallas kernels  97.1 us (92%)
  local copies, waits for them, and re-layouts  5.95 us (6%)
    pallas_call x1, Pallas kernels, on_device(): pl.pallas_call(encode_kernel, out_shape=(jax.ShapeDtypeStruct((2, OWN, D)...  97.1 us
    unnamed x5, local copies, waits for them, and re-layouts  4.77 us

commit v1 on v0

v1 whole, which is shorter than its diff:
```python
import jax
import jax.numpy as jnp
from jax import lax
from jax.experimental import pallas as pl
from jax.experimental.pallas import tpu as pltpu
from jax.sharding import Mesh
from jax.sharding import PartitionSpec as P

D = 1024
HEAD = 64
ROWS = 512
OWN = 256
DP = ("dp_0", "dp_1", "dp_2")
DP_MP = ("dp_0", "dp_1", "dp_2", "mp")
MESH = pl.DeviceIdType.MESH
BF = jnp.bfloat16
TILE = 128
ORDERS = ((2, 1, 0), (1, 0, 2), (0, 2, 1))
BATCHES = ((2, 2, 2), (3, 2, 2), (2, 3, 2), (3, 2, 3), (2, 3, 3), (3, 3, 2), (2, 3, 3))
COUNT = len(BATCHES)
TILES = sum(sum(b) for b in BATCHES)
COLUMNS = TILE * TILES


def place_tiles():
    base = [sum(b[c] for b in BATCHES) for c in range(3)]
    base = [0, base[0], base[0] + base[1]]
    where, spans = [], []
    at = list(base)
    for batch in BATCHES:
        spans.append([at[c] for c in range(3)])
        for c in range(3):
            where += list(range(at[c], at[c] + batch[c]))
            at[c] += batch[c]
    spans.append(at)
    return where, spans


WHERE, SPANS = place_tiles()


def runs(first, tiles):
    found = []
    for t in range(first, first + tiles):
        if found and found[-1][0] + found[-1][1] == WHERE[t]:
            found[-1][1] += 1
        else:
            found.append([WHERE[t], 1])
    return [(a * TILE, n * TILE) for a, n in found]


class Gather:

    def __init__(self, whole, send_sems, recv_sems):
        self.whole, self.send, self.recv = whole, send_sems, recv_sems
        self.me = [lax.axis_index(a) for a in DP]
        self.half = lax.axis_index("mp")
        self.sems = {}
        self.done = set()

    def span(self, group, colour):
        start = SPANS[group[0]][colour] * TILE
        return start, SPANS[group[1]][colour] * TILE - start

    def region(self, colour, phase, coord, start, size):
        at = [None, None, None]
        for i, axis in enumerate(ORDERS[colour]):
            at[axis] = pl.ds(0, 4) if i < phase else (coord if i == phase else self.me[axis])
        return self.whole.at[self.half, at[0], at[1], at[2], :, pl.ds(start, size)]

    def sem(self, key):
        return self.sems.setdefault(key, len(self.sems))

    def copy(self, key, block, device):
        at = self.sem(key)
        pltpu.make_async_remote_copy(
            src_ref=block,
            dst_ref=block,
            send_sem=self.send.at[at],
            recv_sem=self.recv.at[at],
            device_id=device,
            device_id_type=MESH,
        ).start()

    def all_of(self, key):
        group, phase, step = key
        size = sum(self.span(group, c)[1] for c in range(3))
        slots = {"x": 64, "a": 2 * 4 ** phase, "b": 4 ** phase, "d": 3 * 4 ** phase}[step]
        z, y, x = max(slots // 16, 1), min(max(slots // 4, 1), 4), min(slots, 4)
        assert z * y * x == slots
        block = self.whole.at[self.half, pl.ds(0, z), pl.ds(0, y), pl.ds(0, x), :, pl.ds(0, size)]
        at = self.sem(key)
        return pltpu.make_async_remote_copy(
            src_ref=block,
            dst_ref=block,
            send_sem=self.send.at[at],
            recv_sem=self.recv.at[at],
            device_id={"mp": 1 - self.half},
            device_id_type=MESH,
        )

    def wait(self, group, phase, step):
        self.all_of((group, phase, step)).wait_recv()

    def line(self, colour, phase):
        axis = ORDERS[colour][phase]
        mine = self.me[axis]
        return DP[axis], mine, lax.rem(mine + 1, 4), lax.rem(mine + 3, 4)

    def a(self, group, phase):
        for colour in range(3):
            name, mine, right, left = self.line(colour, phase)
            block = self.region(colour, phase, mine, *self.span(group, colour))
            self.copy((group, phase, "a"), block, {name: right})
            self.copy((group, phase, "a"), block, {name: left})
        if phase == 2:
            self.across(group, 0)

    def d(self, group, phase):
        for colour in range(3):
            name, mine, _, _ = self.line(colour, phase)
            block = self.region(colour, phase, mine, *self.span(group, colour))
            for step in (1, 3, 2):
                self.copy((group, phase, "d"), block, {name: lax.rem(mine + step, 4)})

    def b(self, group, phase):
        self.wait(group, phase, "a")
        for colour in range(3):
            name, mine, right, left = self.line(colour, phase)
            start, size = self.span(group, colour)
            first = (size // TILE + colour % 2) // 2 * TILE
            from_left = self.region(colour, phase, left, start, first)
            from_right = self.region(colour, phase, right, start + first, size - first)
            self.copy((group, phase, "b"), from_left, {name: right})
            self.copy((group, phase, "b"), from_right, {name: left})
        if phase == 2:
            self.across(group, 1)
            self.across(group, 3)

    def across(self, group, step):
        for colour in range(3):
            coord = lax.rem(self.me[ORDERS[colour][2]] + step, 4)
            block = self.region(colour, 2, coord, *self.span(group, colour))
            self.copy((group, 2, "x"), block, {"mp": 1 - self.half})

    def finish(self, group):
        self.wait(group, 2, "b")
        self.across(group, 2)

    def arrived(self, group):
        self.wait(group, 2, "x")

    def drain(self):
        for key in self.sems:
            self.all_of(key).wait_send()


def layer_norm(inputs, gains):
    average = jnp.mean(inputs, axis=-1, keepdims=True)
    centred = inputs - average
    spread = jnp.mean(centred * centred, axis=-1, keepdims=True)
    return centred * lax.rsqrt(spread + 1e-06) * gains


def dot(a, b):
    return jnp.dot(a, b, preferred_element_type=jnp.float32)


def dot_t(a, b):
    return lax.dot_general(a, b, (((1,), (1,)), ((), ())), preferred_element_type=jnp.float32)


def encode_kernel(
    counts,
    owner,
    pixels,
    embed,
    w_qkv,
    w_out,
    w_up,
    w_down,
    gain1,
    gain2,
    aims,
    encoded,
    loss,
    whole,
    picture,
    targets,
    outcome,
    spread,
    tokens,
    normed,
    queries,
    key_rows,
    value_rows,
    attended,
    total,
    sending,
    by_image,
    sums,
    send_sems,
    recv_sems,
    end_send,
    end_recv,
    local_sems,
):
    half = lax.axis_index("mp")
    other = 1 - half
    me = [lax.axis_index(a) for a in DP]
    get_picture = pltpu.make_async_copy(pixels, picture, local_sems.at[0])
    get_targets = pltpu.make_async_copy(aims, targets, local_sems.at[1])
    get_picture.start()
    get_targets.start()
    barrier = pltpu.get_barrier_semaphore()
    for name, mine in zip(DP, me):
        for step in (1, 2, 3):
            pl.semaphore_signal(
                barrier, inc=1, device_id={name: lax.rem(mine + step, 4)}, device_id_type=MESH
            )
    pl.semaphore_signal(barrier, inc=1, device_id={"mp": other}, device_id_type=MESH)

    def place(first, value):
        at = 0
        for start, size in runs(first, value.shape[1] // TILE):
            whole[half, me[0], me[1], me[2], :, pl.ds(start, size)] = value[:, at : at + size]
            at += size

    padded = [embed[...].astype(jnp.float32), jnp.zeros((4, 512), jnp.float32)]
    place(0, jnp.concatenate(padded, 0).astype(BF))
    for i in range(3):
        place(4 + 4 * i, w_qkv[i])
    place(16, w_out[...])
    for i in range(4):
        place(20 + 8 * i, w_up[:, pl.ds(512 * i, 512)])
        place(24 + 8 * i, w_down[:, pl.ds(512 * i, 512)])
    from_px = lax.broadcasted_iota(jnp.int32, (768, D), 0)
    column = lax.broadcasted_iota(jnp.int32, (768, D), 1)
    within = lax.bitwise_and(column, 15)
    to_px = lax.shift_right_logical(column, 4) * 12 + within
    pick = jnp.where((from_px == to_px) & (within < 12), 1.0, 0.0).astype(BF)
    pl.semaphore_wait(barrier, 10)
    g = Gather(whole, send_sems, recv_sems)

    def weights(h, first, tiles):
        parts = [whole[h, :, :, :, :, pl.ds(a, n)].reshape(D, n) for a, n in runs(first, tiles)]
        return parts[0] if len(parts) == 1 else jnp.concatenate(parts, axis=1)

    one = [(i, i + 1) for i in range(COUNT)]
    head, tail, second, third, fourth = (0, 3), (3, 7), (1, 3), (3, 5), (5, 7)
    g.d(head, 0)
    g.a(tail, 0)
    get_picture.wait()
    spread[...] = dot(picture[...], pick).astype(BF)
    g.wait(head, 0, "d")
    g.d(one[0], 1)
    g.a(second, 1)
    g.b(tail, 0)
    g.wait(one[0], 1, "d")
    g.a(one[0], 2)
    g.b(second, 1)
    g.wait(tail, 0, "b")
    g.a(third, 1)
    g.b(one[0], 2)
    g.wait(second, 1, "b")
    g.a(one[1], 2)
    g.a(one[2], 2)
    g.b(third, 1)
    g.a(fourth, 1)
    g.finish(one[0])
    g.b(one[1], 2)
    g.wait(third, 1, "b")
    g.a(one[3], 2)
    g.arrived(one[0])
    for h in range(2):
        tokens[:, pl.ds(512 * h, 512)] = dot(spread[...], weights(h, 0, 4)).astype(BF)
    normed[...] = layer_norm(tokens[...].astype(jnp.float32), gain1[...]).astype(BF)
    g.b(one[2], 2)
    g.b(fourth, 1)
    g.a(one[4], 2)
    g.finish(one[1])

    def project(ref, first, factor):
        for h in range(2):
            part = dot(normed[...], weights(h, first, 4))
            if factor != 1.0:
                part = part * factor
            part = part.astype(BF)
            for j in range(4):
                ref[4 * h + j] = part[:, 128 * j : 128 * (j + 1)]

    g.arrived(one[1])
    project(queries, 4, HEAD ** (-0.5))
    project(key_rows, 8, 1.0)
    g.finish(one[2])
    g.b(one[3], 2)
    g.wait(fourth, 1, "b")
    g.a(one[5], 2)
    g.arrived(one[2])
    project(value_rows, 12, 1.0)
    length = counts[0, half]
    key_id = lax.broadcasted_iota(jnp.int32, (1, ROWS), 1)
    bias = jnp.where(key_id < length, 0.0, -1e30)
    low = lax.broadcasted_iota(jnp.int32, (ROWS, 128), 1) < HEAD

    def pair(i, carry):
        q, k, v = queries[i], key_rows[i], value_rows[i]
        none, ones = jnp.zeros_like(q), jnp.ones_like(v)

        def head_of(q_part, v_part):
            scores = dot_t(q_part, k) + bias
            expo = jnp.exp(scores - jnp.max(scores, axis=-1, keepdims=True))
            return dot(expo.astype(BF), v_part)

        first = head_of(jnp.where(low, q, none), jnp.where(low, v, ones))
        second = head_of(jnp.where(low, none, q), jnp.where(low, ones, v))
        values = jnp.where(low, first, second)
        row_sums = pltpu.roll(jnp.where(low, second, first), HEAD, 1)
        attended[i] = (values / row_sums).astype(BF)
        return carry

    lax.fori_loop(0, 2, pair, 0)
    g.finish(one[3])
    g.b(one[4], 2)
    g.a(one[6], 2)
    lax.fori_loop(2, 5, pair, 0)
    g.finish(one[4])
    g.b(one[5], 2)
    lax.fori_loop(5, 8, pair, 0)
    g.finish(one[5])
    residual = tokens[...].astype(jnp.float32)
    for h in range(2):
        mixed = jnp.concatenate([attended[4 * h + j] for j in range(4)], axis=1)
        residual = residual + dot_t(mixed, weights(h, 16, 4))
    total[...] = residual
    normed[...] = layer_norm(residual, gain2[...]).astype(BF)

    def mlp(rows, quarter):
        found = None
        for h in range(2):
            hidden = dot(normed[rows, :], weights(h, 20 + 8 * quarter, 4))
            hidden = hidden * 0.5 * (1.0 + lax.erf(hidden * (0.5**0.5)))
            part = dot_t(hidden.astype(BF), weights(h, 24 + 8 * quarter, 4))
            found = part if found is None else found + part
        return found

    everything = pl.ds(0, ROWS)
    g.b(one[6], 2)
    g.arrived(one[3])
    total[...] += mlp(everything, 0)
    g.arrived(one[4])
    total[...] += mlp(everything, 1)
    g.finish(one[6])
    g.arrived(one[5])
    total[...] += mlp(everything, 2)
    g.arrived(one[6])
    for piece, mine in ((other, False), (half, True)):
        rows = pl.ds(pl.multiple_of(piece * OWN, OWN), OWN)
        result = (total[rows, :] + mlp(rows, 3)).astype(BF)
        if mine:
            by_image[half] = result
        else:
            sending[...] = result
            exchange = pltpu.make_async_remote_copy(
                src_ref=sending,
                dst_ref=by_image.at[half],
                send_sem=end_send.at[0],
                recv_sem=end_recv.at[0],
                device_id={"mp": other},
                device_id_type=MESH,
            )
            exchange.start()
    get_targets.wait()
    exchange.wait_recv()
    row_id = half * OWN + lax.broadcasted_iota(jnp.int32, (OWN, 1), 0)
    squares = jnp.zeros((8, 128), jnp.float32)
    number = jnp.zeros((8, 128), jnp.float32)
    for step in range(2):
        source = owner[0, step]
        valid = jnp.where(source == 0, counts[0, 0], counts[0, 1])
        rows = jnp.where(source == 0, by_image[0].astype(jnp.float32), by_image[1].astype(jnp.float32))
        outcome[step] = rows.astype(BF)
        misfit = rows - targets[step].astype(jnp.float32)
        misfit = jnp.where(row_id < valid, misfit * misfit, 0.0)
        squares = squares + misfit.reshape(OWN // 8, 8, 8, 128).sum(axis=(0, 2))
        number = number + jnp.clip(valid - half * OWN, 0, OWN).astype(jnp.float32)
    both = jnp.concatenate([squares, number], 0)
    at = 1
    lines = [("mp", 2, half)] + [(name, 4, mine) for name, mine in zip(DP, me)]
    for stage, (name, members, mine) in enumerate(lines):
        sums[stage, mine] = both
        sent = []
        for step in range(1, members):
            made = pltpu.make_async_remote_copy(
                src_ref=sums.at[stage, mine],
                dst_ref=sums.at[stage, mine],
                send_sem=end_send.at[at],
                recv_sem=end_recv.at[at],
                device_id={name: lax.rem(mine + step, members)},
                device_id_type=MESH,
            )
            made.start()
            sent.append(made)
            at += 1
        if stage == 0:
            put = pltpu.make_async_copy(outcome, encoded, local_sems.at[2])
            put.start()
            g.drain()
            exchange.wait_send()
        for made in sent:
            made.wait_recv()
        both = sums[stage, 0]
        for member in range(1, members):
            both = both + sums[stage, member]
        for made in sent:
            made.wait_send()
    mean = jnp.sum(both[:8]) / (D * jnp.max(both[8:]))
    loss[...] = jnp.full((1, 1), mean, jnp.float32)
    put.wait()


N_SEMS = 40


def on_device(
    pixels, counts, owner, embed_weight, w_qkv, w_out, w_up, w_down, ln1_gain, ln2_gain, targets
):
    vmem = pl.BlockSpec(memory_space=pltpu.VMEM)
    smem = pl.BlockSpec(memory_space=pltpu.SMEM)
    hbm = pl.BlockSpec(memory_space=pl.ANY)
    encoded, loss = pl.pallas_call(
        encode_kernel,
        out_shape=(
            jax.ShapeDtypeStruct((2, OWN, D), BF),
            jax.ShapeDtypeStruct((1, 1), jnp.float32),
        ),
        in_specs=[smem, smem, hbm] + [vmem] * 7 + [hbm],
        out_specs=(hbm, vmem),
        scratch_shapes=[
            pltpu.VMEM((2, 4, 4, 4, 16, COLUMNS), BF),
            pltpu.VMEM((ROWS, 768), BF),
            pltpu.VMEM((2, OWN, D), BF),
            pltpu.VMEM((2, OWN, D), BF),
            pltpu.VMEM((ROWS, D), BF),
            pltpu.VMEM((ROWS, D), BF),
            pltpu.VMEM((ROWS, D), BF),
            pltpu.VMEM((8, ROWS, 128), BF),
            pltpu.VMEM((8, ROWS, 128), BF),
            pltpu.VMEM((8, ROWS, 128), BF),
            pltpu.VMEM((8, ROWS, 128), BF),
            pltpu.VMEM((ROWS, D), jnp.float32),
            pltpu.VMEM((OWN, D), BF),
            pltpu.VMEM((2, OWN, D), BF),
            pltpu.VMEM((4, 4, 16, 128), jnp.float32),
            pltpu.SemaphoreType.DMA((N_SEMS,)),
            pltpu.SemaphoreType.DMA((N_SEMS,)),
            pltpu.SemaphoreType.DMA((11,)),
            pltpu.SemaphoreType.DMA((11,)),
            pltpu.SemaphoreType.DMA((3,)),
        ],
        compiler_params=pltpu.CompilerParams(
            collective_id=0, has_side_effects=True, vmem_limit_bytes=64 * 1024 * 1024 - 65536
        ),
        name="encode",
    )(
        counts,
        owner,
        pixels[0],
        embed_weight,
        w_qkv,
        w_out.T,
        w_up,
        w_down.T,
        ln1_gain[None],
        ln2_gain[None],
        targets[0],
    )
    return (encoded[None], loss[0, 0])


def solution(mesh):
    split = Mesh(mesh.devices.reshape(4, 4, 4, mesh.shape["mp"]), ("dp_0", "dp_1", "dp_2", "mp"))
    return jax.shard_map(
        on_device,
        mesh=split,
        in_specs=(
            P(DP_MP, None, None),
            P(DP, None),
            P(DP, None),
            P(DP, "mp"),
            P(None, DP, "mp"),
            P("mp", DP),
            P(DP, "mp"),
            P("mp", DP),
            P(),
            P(),
            P(DP, None, "mp", None),
        ),
        out_specs=(P(DP, None, "mp", None), P()),
        check_vma=False,
    )
```

time: 105 us -> 90.9 us (0.87)
  Pallas kernels: 97.1 us -> 84.8 us
  local copies, waits for them, and re-layouts: 5.95 us -> 2.26 us
  between operations: 0.65 us -> 2.33 us
    pallas_call x1, Pallas kernels: 97.1 us -> 84.8 us  [on_device(): pl.pallas_call(encode_kernel, out_shape=(jax.ShapeDtypeStruct((2, OWN, D)...]
    unnamed x5 -> x1, local copies, waits for them, and re-layouts: 4.77 us -> 2.26 us
    slice x1 -> x0, local copies, waits for them, and re-layouts: 1.18 us -> none  [on_device(): return (encoded[None], loss[0, 0])]
where the time goes in v1:
time: 90.9 us; the launch traced here: 89.4 us
  Pallas kernels  84.8 us (93%)
  between operations  2.33 us (3%)
  local copies, waits for them, and re-layouts  2.26 us (2%)
    pallas_call x1, Pallas kernels, on_device(): pl.pallas_call(encode_kernel, out_shape=(jax.ShapeDtypeStruct((2, OWN, D)...  84.8 us
    unnamed x1, local copies, waits for them, and re-layouts  2.26 us

profile of v1, /device:TPU:1, one launch (start us, length us, event | category | flops | bytes accessed | tf_op | source)
XLA Modules:
  0.0 89.4 jit_solution(17811916659938943292)
XLA Ops:
  0.6 84.8 %encode.1 = (bf16[2,256,1024]{2,1,0:T(8,128)(2,1)}, f32[1,1]{1,0:T(1,128)}) custom-call(s32[1,2]{1,0:T(1,128)} %counts.1, s32[1,2]{1,0:T(1,128)} %owner.1, bf16[512,768]{1,0:T(8,128)(2,1)} %bitcast.10, bf16[12,512]{1,0:T(8,128)(2,1)} %embed.1, bf16[3,16,512]{2,1,0:T(8,128)(2,1)} %w_qkv.1, bf16[16,512]{1,0:T(8,128)(2,1)} %bitcast.12, bf16[16,2048]{1,0:T(8,128)(2,1)} %w_up.1, ...), custom_call_target="tpu_custom_call" | custom-call | tf_op jit(solution)/shard_map/encode/pallas_call | solution.py:431
  85.4 2.3 %copy.15 = bf16[1,2,256,1024]{3,2,1,0:T(8,128)(2,1)} copy(bf16[1,2,256,1024]{3,2,1,0:T(8,128)(2,1)} %bitcast.9) | data formatting | bytes 2097152
